TPU v7x, 32 devices: a whole 2x2x4 slice. The times are simulated.
32 devices in a mesh: dp: 8 (over y, x, core), tensor: 4 (over z).
Axes of the slice: x: 2, y: 2, z: 4, core: 2. Of those that a mesh axis runs over, the one named last changes fastest.
Arguments:
- tokens: bfloat16 [16384, 1024], P(('dp', 'tensor')), may hold values from -6 to 6
- lengths: int32 [8], P('dp'), may hold values from 120 to 2048, as said below
- ln1_gain: float32 [1024], replicated, may hold values from 0.1 to 1.9
- ln1_bias: float32 [1024], replicated, may hold values from -3 to 3
- w_query: bfloat16 [1024, 1024], P(None, 'tensor'), may hold values from -0.25 to 0.25
- w_key: bfloat16 [1024, 1024], P(None, 'tensor'), may hold values from -0.25 to 0.25
- w_value: bfloat16 [1024, 1024], P(None, 'tensor'), may hold values from -0.1875 to 0.1875
- w_out: bfloat16 [1024, 1024], P('tensor'), may hold values from -0.75 to 0.75
- ln2_gain: float32 [1024], replicated, may hold values from 0.1 to 1.9
- ln2_bias: float32 [1024], replicated, may hold values from -3 to 3
- w_gate: bfloat16 [1024, 4096], P(None, 'tensor'), may hold values from -0.1875 to 0.1875
- w_up: bfloat16 [1024, 4096], P(None, 'tensor'), may hold values from -0.1875 to 0.1875
- down_weight: bfloat16 [4096, 1024], P('tensor'), may hold values from -0.125 to 0.125
- cotangent: bfloat16 [16384, 1024], P(('dp', 'tensor')), may hold values from -6 to 6
Outputs:
- output: bfloat16 [16384, 1024], P(('dp', 'tensor'))
- input_grad: float32 [16384, 1024], P(('dp', 'tensor'))
- ln1_gain_grad: float32 [1024], replicated
- ln1_bias_grad: float32 [1024], replicated
- query_grad: float32 [1024, 1024], P(None, 'tensor')
- key_grad: float32 [1024, 1024], P(None, 'tensor')
- value_grad: float32 [1024, 1024], P(None, 'tensor')
- out_grad: float32 [1024, 1024], P('tensor')
- ln2_gain_grad: float32 [1024], replicated
- ln2_bias_grad: float32 [1024], replicated
- gate_grad: float32 [1024, 4096], P(None, 'tensor')
- up_grad: float32 [1024, 4096], P(None, 'tensor')
- down_grad: float32 [4096, 1024], P('tensor')
Inputs may be any that keep to these rules, and one draw needn't show every extreme that they name: `lengths`: real tokens of each window; every draw has a window of exactly 2048 and one of exactly 120.
All inputs are finite; a program needn't handle non-finite values.
Results may differ from a plain program's by a relative error of at most 0.023.
The roundings to bfloat16 on the way count: a program that leaves them out, or rounds other values in their place, can miss the bound.
Values may be sent and summed in bfloat16 or wider, within the bound.
A program may use at most 192 MiB of HBM per device.

v0:
```python
import math
import jax
import jax.numpy as jnp
from jax import lax
from jax.sharding import PartitionSpec as P

HD = 64
eps = 1e-05


def norm_parts(values, gain, shift):
    centre = jnp.mean(values, axis=-1, keepdims=True)
    centred = values - centre
    inverse = lax.rsqrt(jnp.mean(centred * centred, axis=-1, keepdims=True) + eps)
    scaled = centred * inverse
    return (scaled * gain + shift, scaled, inverse)


def norm_back(upstream, scaled, inverse, gain):
    through = upstream * gain
    inner = (
        through
        - jnp.mean(through, axis=-1, keepdims=True)
        - scaled * jnp.mean(through * scaled, axis=-1, keepdims=True)
    )
    return (inverse * inner, jnp.sum(upstream * scaled, axis=0), jnp.sum(upstream, axis=0))


def angle_tables(length, width):
    half_width = width // 2
    freqs = 10000.0 ** (-(jnp.arange(half_width, dtype=jnp.float32) * 2.0 / width))
    angles = jnp.arange(length, dtype=jnp.float32)[:, None] * freqs[None, :]
    return (jnp.cos(angles), jnp.sin(angles))


def rotate(values, cosine, sine):
    half_width = values.shape[-1] // 2
    first = values[..., :half_width]
    second = values[..., half_width:]
    return jnp.concatenate(
        [first * cosine - second * sine, second * cosine + first * sine], axis=-1
    )


def unrotate(values, cosine, sine):
    half_width = values.shape[-1] // 2
    first = values[..., :half_width]
    second = values[..., half_width:]
    return jnp.concatenate(
        [first * cosine + second * sine, second * cosine - first * sine], axis=-1
    )


def scores_block(query_block, key_rows, limit, factor):
    raw = (
        jnp.einsum("qhe,khe->hqk", query_block, key_rows, preferred_element_type=jnp.float32)
        * factor
    )
    live = lax.iota(jnp.int32, key_rows.shape[0]) < limit
    return jnp.where(live[None, None, :], raw, -1e30)


def attend(query, keys, values, lengths, block):
    windows, length, heads, depth = query.shape
    per_window = length // block
    factor = 1.0 / math.sqrt(depth)

    def one_block(index):
        window = index // per_window
        start = index % per_window * block
        query_win = lax.dynamic_index_in_dim(query, window, 0, keepdims=False)
        query_block = lax.dynamic_slice_in_dim(query_win, start, block, 0)
        key_rows = lax.dynamic_index_in_dim(keys, window, 0, keepdims=False)
        value_rows = lax.dynamic_index_in_dim(values, window, 0, keepdims=False)
        limit = lax.dynamic_index_in_dim(lengths, window, 0, keepdims=False)
        scores = scores_block(query_block, key_rows, limit, factor)
        peak = jnp.max(scores, axis=-1, keepdims=True)
        expos = jnp.exp(scores - peak)
        total = jnp.sum(expos, axis=-1, keepdims=True)
        probs_low = (expos / total).astype(jnp.bfloat16)
        context = jnp.einsum(
            "hqk,khe->qhe", probs_low, value_rows, preferred_element_type=jnp.float32
        ).astype(jnp.bfloat16)
        return (context, (peak + jnp.log(total))[..., 0])

    context, logsum = lax.map(one_block, jnp.arange(windows * per_window))
    return (context.reshape(query.shape), logsum.reshape(windows, per_window, heads, block))


def attend_back(query, keys, values, grad_context, logsum, lengths, block):
    windows, length, heads, depth = query.shape
    per_window = length // block
    factor = 1.0 / math.sqrt(depth)

    def one_window(window):
        query_win = lax.dynamic_index_in_dim(query, window, 0, keepdims=False)
        key_rows = lax.dynamic_index_in_dim(keys, window, 0, keepdims=False)
        value_rows = lax.dynamic_index_in_dim(values, window, 0, keepdims=False)
        grad_win = lax.dynamic_index_in_dim(grad_context, window, 0, keepdims=False)
        logsum_win = lax.dynamic_index_in_dim(logsum, window, 0, keepdims=False)
        limit = lax.dynamic_index_in_dim(lengths, window, 0, keepdims=False)

        def one_step(carry, step):
            key_grad, value_grad = carry
            start = step * block
            query_block = lax.dynamic_slice_in_dim(query_win, start, block, 0)
            grad_block = lax.dynamic_slice_in_dim(grad_win, start, block, 0)
            scores = scores_block(query_block, key_rows, limit, factor)
            level = lax.dynamic_index_in_dim(logsum_win, step, 0, keepdims=False)
            probs = jnp.exp(scores - level[:, :, None])
            probs_low = probs.astype(jnp.bfloat16)
            context = jnp.einsum(
                "hqk,khe->qhe", probs_low, value_rows, preferred_element_type=jnp.float32
            ).astype(jnp.bfloat16)
            grad_probs = jnp.einsum(
                "qhe,khe->hqk", grad_block, value_rows, preferred_element_type=jnp.float32
            )
            inner = jnp.sum(probs * grad_probs, axis=-1, keepdims=True)
            grad_scores = (probs * (grad_probs - inner)).astype(jnp.bfloat16)
            query_grad = (
                jnp.einsum(
                    "hqk,khe->qhe", grad_scores, key_rows, preferred_element_type=jnp.float32
                )
                * factor
            )
            key_grad = (
                key_grad
                + jnp.einsum(
                    "hqk,qhe->khe", grad_scores, query_block, preferred_element_type=jnp.float32
                )
                * factor
            )
            value_grad = value_grad + jnp.einsum(
                "hqk,qhe->khe", probs_low, grad_block, preferred_element_type=jnp.float32
            )
            return ((key_grad, value_grad), (query_grad, context))

        zero_rows = jnp.zeros(key_rows.shape, jnp.float32)
        (key_grad, value_grad), (query_grad, context) = lax.scan(
            one_step, (zero_rows, zero_rows), jnp.arange(per_window)
        )
        return (
            query_grad.reshape(key_rows.shape),
            key_grad,
            value_grad,
            context.reshape(key_rows.shape),
        )

    return lax.map(one_window, jnp.arange(windows))


def on_device(
    tokens,
    lengths,
    ln1_gain,
    ln1_bias,
    w_query,
    w_key,
    w_value,
    w_out,
    ln2_gain,
    ln2_bias,
    w_gate,
    w_up,
    down_weight,
    cotangent,
):
    local_rows = tokens.shape[0]
    group_rows = local_rows * lax.axis_size("tensor")
    windows = lengths.shape[0]
    length = group_rows // windows
    block = min(512, length)
    heads_here = w_query.shape[1] // HD
    width_here = heads_here * HD
    hidden_here = w_gate.shape[1]
    row_ids = lax.axis_index("tensor") * local_rows + lax.iota(jnp.int32, local_rows)
    window_ids = row_ids // length
    limits = jnp.sum(
        jnp.where(
            window_ids[:, None] == lax.iota(jnp.int32, windows)[None, :], lengths[None, :], 0
        ),
        axis=1,
    )
    valid = (row_ids % length < limits)[:, None]
    cosine, sine = angle_tables(length, HD)
    cosine = cosine[None, :, None, :]
    sine = sine[None, :, None, :]
    w_qkv = jnp.concatenate([w_query, w_key, w_value], axis=1)
    w_pair = jnp.concatenate([w_gate, w_up], axis=1)

    def project(rows_full):
        mixed = jnp.dot(rows_full, w_qkv, preferred_element_type=jnp.float32)
        shaped = mixed.reshape(windows, length, 3, heads_here, HD)
        query = rotate(shaped[:, :, 0], cosine, sine).astype(jnp.bfloat16)
        keys = rotate(shaped[:, :, 1], cosine, sine).astype(jnp.bfloat16)
        values = shaped[:, :, 2].astype(jnp.bfloat16)
        return (query, keys, values)

    def gated(rows_full):
        both = jnp.dot(rows_full, w_pair, preferred_element_type=jnp.float32)
        gate = both[:, :hidden_here]
        upper = both[:, hidden_here:]
        sigma = jax.nn.sigmoid(gate)
        return (gate, upper, sigma, (gate * sigma * upper).astype(jnp.bfloat16))

    inputs = tokens.astype(jnp.float32)
    normed1, scaled1, inverse1 = norm_parts(inputs, ln1_gain, ln1_bias)
    attn_in = normed1.astype(jnp.bfloat16)
    attn_rows = lax.all_gather(attn_in, "tensor", axis=0, tiled=True)
    query, keys, values = project(attn_rows)
    context, logsum = attend(query, keys, values, lengths, block)
    context_rows = context.reshape(group_rows, width_here)
    picked = context_rows
    attn_out = lax.psum_scatter(
        jnp.dot(picked, w_out, preferred_element_type=jnp.float32)
        .astype(jnp.bfloat16)
        .astype(jnp.float32)
        .astype(jnp.bfloat16),
        "tensor",
        scatter_dimension=0,
        tiled=True,
    ).astype(jnp.float32)
    middle = inputs + attn_out
    normed2, scaled2, inverse2 = norm_parts(middle, ln2_gain, ln2_bias)
    ffn_in = normed2.astype(jnp.bfloat16)
    ffn_rows = lax.all_gather(ffn_in, "tensor", axis=0, tiled=True)
    hidden_activations = gated(ffn_rows)[3]
    picked = hidden_activations
    ffn_out = lax.psum_scatter(
        jnp.dot(picked, down_weight, preferred_element_type=jnp.float32)
        .astype(jnp.bfloat16)
        .astype(jnp.float32)
        .astype(jnp.bfloat16),
        "tensor",
        scatter_dimension=0,
        tiled=True,
    ).astype(jnp.float32)
    output = jnp.where(valid, middle + ffn_out, 0.0).astype(jnp.bfloat16)
    grad_out = jnp.where(valid, cotangent.astype(jnp.float32), 0.0)
    grad_branch = lax.all_gather(grad_out.astype(jnp.bfloat16), "tensor", axis=0, tiled=True)
    ffn_back = lax.all_gather(ffn_in, "tensor", axis=0, tiled=True)
    gate, upper, sigma, hidden_back = gated(ffn_back)
    down_grad = jnp.einsum(
        "rf,rd->fd", hidden_back, grad_branch, preferred_element_type=jnp.float32
    )
    grad_hidden = jnp.einsum(
        "rd,fd->rf", grad_branch, down_weight, preferred_element_type=jnp.float32
    )
    grad_gate = grad_hidden * upper * sigma * (1.0 + gate * (1.0 - sigma))
    grad_upper = grad_hidden * gate * sigma
    grad_pair = jnp.concatenate([grad_gate, grad_upper], axis=1).astype(jnp.bfloat16)
    pair_grad = jnp.einsum("rd,rf->df", ffn_back, grad_pair, preferred_element_type=jnp.float32)
    gate_grad = pair_grad[:, :hidden_here]
    up_grad = pair_grad[:, hidden_here:]
    picked = grad_pair
    grad_ffn_in = lax.psum_scatter(
        jnp.einsum("rf,df->rd", picked, w_pair, preferred_element_type=jnp.float32)
        .astype(jnp.bfloat16)
        .astype(jnp.float32)
        .astype(jnp.bfloat16),
        "tensor",
        scatter_dimension=0,
        tiled=True,
    ).astype(jnp.float32)
    grad_norm2, gain2_grad, shift2_grad = norm_back(grad_ffn_in, scaled2, inverse2, ln2_gain)
    grad_middle = grad_out + grad_norm2
    grad_attn = lax.all_gather(grad_middle.astype(jnp.bfloat16), "tensor", axis=0, tiled=True)
    attn_back = lax.all_gather(attn_in, "tensor", axis=0, tiled=True)
    query, keys, values = project(attn_back)
    grad_context = jnp.einsum(
        "rd,cd->rc", grad_attn, w_out, preferred_element_type=jnp.float32
    ).astype(jnp.bfloat16)
    grad_context = grad_context.reshape(windows, length, heads_here, HD)
    query_back, key_back, value_back, context_back = attend_back(
        query, keys, values, grad_context, logsum, lengths, block
    )
    out_grad = jnp.einsum(
        "rc,rd->cd",
        context_back.reshape(group_rows, width_here),
        grad_attn,
        preferred_element_type=jnp.float32,
    )
    grad_mixed = jnp.concatenate(
        [
            unrotate(query_back, cosine, sine).reshape(group_rows, width_here),
            unrotate(key_back, cosine, sine).reshape(group_rows, width_here),
            value_back.reshape(group_rows, width_here),
        ],
        axis=1,
    ).astype(jnp.bfloat16)
    qkv_grad = jnp.einsum("rd,rc->dc", attn_back, grad_mixed, preferred_element_type=jnp.float32)
    query_grad = qkv_grad[:, :width_here]
    key_grad = qkv_grad[:, width_here : 2 * width_here]
    value_grad = qkv_grad[:, 2 * width_here :]
    picked = grad_mixed
    grad_attn_in = lax.psum_scatter(
        jnp.einsum("rc,dc->rd", picked, w_qkv, preferred_element_type=jnp.float32)
        .astype(jnp.bfloat16)
        .astype(jnp.float32)
        .astype(jnp.bfloat16),
        "tensor",
        scatter_dimension=0,
        tiled=True,
    ).astype(jnp.float32)
    grad_norm1, gain1_grad, shift1_grad = norm_back(grad_attn_in, scaled1, inverse1, ln1_gain)
    input_grad = grad_middle + grad_norm1
    query_grad, key_grad, value_grad, out_grad, gate_grad, up_grad, down_grad = (
        lax.psum(query_grad.astype(jnp.bfloat16), "dp").astype(jnp.float32),
        lax.psum(key_grad.astype(jnp.bfloat16), "dp").astype(jnp.float32),
        lax.psum(value_grad.astype(jnp.bfloat16), "dp").astype(jnp.float32),
        lax.psum(out_grad.astype(jnp.bfloat16), "dp").astype(jnp.float32),
        lax.psum(gate_grad.astype(jnp.bfloat16), "dp").astype(jnp.float32),
        lax.psum(up_grad.astype(jnp.bfloat16), "dp").astype(jnp.float32),
        lax.psum(down_grad.astype(jnp.bfloat16), "dp").astype(jnp.float32),
    )
    gain1_grad, shift1_grad, gain2_grad, shift2_grad = lax.psum(
        (gain1_grad, shift1_grad, gain2_grad, shift2_grad), ("dp", "tensor")
    )
    return (
        output,
        input_grad,
        gain1_grad,
        shift1_grad,
        query_grad,
        key_grad,
        value_grad,
        out_grad,
        gain2_grad,
        shift2_grad,
        gate_grad,
        up_grad,
        down_grad,
    )


def solution(mesh):
    return jax.shard_map(
        on_device,
        mesh=mesh,
        in_specs=(
            P(("dp", "tensor"), None),
            P("dp"),
            P(),
            P(),
            P(None, "tensor"),
            P(None, "tensor"),
            P(None, "tensor"),
            P("tensor", None),
            P(),
            P(),
            P(None, "tensor"),
            P(None, "tensor"),
            P("tensor", None),
            P(("dp", "tensor"), None),
        ),
        out_specs=(
            P(("dp", "tensor"), None),
            P(("dp", "tensor"), None),
            P(),
            P(),
            P(None, "tensor"),
            P(None, "tensor"),
            P(None, "tensor"),
            P("tensor", None),
            P(),
            P(),
            P(None, "tensor"),
            P(None, "tensor"),
            P("tensor", None),
        ),
        check_vma=False,
    )
```

profile of v0, /device:TPU:0, one launch (start us, length us, event | category | flops | bytes accessed | tf_op | source)
XLA Modules:
  0.0 1286.7 jit_solution(5398323214661166941)
XLA Ops:
  18.6 78.9 %all-gather.5.cloned.1.call-done = bf16[2048,1024]{1,0:T(8,128)(2,1)} async-done(((bf16[512,1024]{1,0:T(8,128)(2,1)}), bf16[2048,1024]{1,0:T(8,128)(2,1)}) %all-gather.5.cloned.1.call-update) | async-done | bytes 4194320 | tf_op jit(solution)/shard_map/all_gather | solution.py:209
  97.4 5.8 fusion.82
  108.8 64.1 %while.44 = (s32[]{:T(128)}, bf16[4,512,4,64]{1,3,2,0:T(8,128)(2,1)}, f32[4,4,512]{2,1,0:T(4,128)S(1)}, s32[1]{0:T(128)}, s32[4]{0:T(128)S(1)}, /*index=5*/bf16[...) while((s32[]{:T(128)}, ...), condition=%wide.region_5.6_spmd, body=%wide.region_2.5_spmd.sunk | while | flops 1124204544 | bytes 57221472 | solution.py:86
  115.6 3.7 fusion.132
  119.3 5.5 fusion.133
  131.6 3.7 fusion.132
  135.3 5.5 fusion.133
  147.6 3.7 fusion.132
  151.4 5.5 fusion.133
  163.6 3.7 fusion.132
  167.4 5.5 fusion.133
  178.7 10.1 all-gather.7.cloned.1.call-start
  188.8 65.3 %reduce-scatter.5.cloned.1.call-done = bf16[512,1024]{1,0:T(8,128)(2,1)} async-done(((bf16[2048,1024]{1,0:T(8,128)(2,1)}), bf16[512,1024]{1,0:T(8,128)(2,1)}) %reduce-scatter.5.cloned.1.call-update) | async-done | bytes 1048592 | tf_op jit(solution)/shard_map/reduce_scatter | solution.py:214
  267.0 73.5 %all-gather.7.cloned.1.call-done = bf16[2048,1024]{1,0:T(8,128)(2,1)} async-done(((bf16[512,1024]{1,0:T(8,128)(2,1)}), bf16[2048,1024]{1,0:T(8,128)(2,1)}) %all-gather.7.cloned.1.call-update) | async-done | bytes 4194320 | tf_op jit(solution)/shard_map/all_gather | solution.py:226
  340.5 15.2 %fusion.83 = f32[2048,2048]{0,1:T(8,128)} fusion(bf16[2048,1024]{1,0:T(8,128)(2,1)} %all-gather.7.cloned.1.call-done, bf16[1024,2048]{1,0:T(8,128)(2,1)} %constant_dynamic-update-slice_fusion.3), kind=kOutput, calls=%fused_computation.160 | convolution fusion | flops 8589934592 | bytes 25165824 | tf_op jit(solution)/shard_map/dot_general | solution.py:200
  355.7 66.2 %all-gather.9.cloned.1.call-done = bf16[2048,1024]{1,0:T(8,128)(2,1)} async-done(((bf16[512,1024]{1,0:T(8,128)(2,1)}), bf16[2048,1024]{1,0:T(8,128)(2,1)}) %all-gather.9.cloned.1.call-update) | async-done | bytes 4194320 | tf_op jit(solution)/shard_map/all_gather | solution.py:240
  421.9 13.3 %multiply_convert_fusion.2 = (bf16[2048,1024]{0,1:T(8,128)(2,1)S(1)}, bf16[2048,1024]{0,1:T(8,128)(2,1)S(1)}, bf16[2048,1024]{0,1:T(8,128)(2,1)}) fusion(f32[2048,2048]{0,1:T(8,128)} %fusion.83, bf16[2048,1024]{1,0:T(8,128)(2,1)} %all-gather.9.cloned.1.call-done, bf16[1024,1024]{1,0:T(8,128)(2,1)S(1)} %copy-done), kind=kOutput, calls=%fused_computation.51 | convolution fusion | flops 4328521728 | bytes 35651584 | tf_op jit(solution)/shard_map/rd,fd->rf/dot_general | solution.py:246
  438.5 12.1 fusion.39
  450.7 8.7 convolution_convert_fusion.3
  459.5 66.6 %reduce-scatter.9.cloned.1.call-done = bf16[512,1024]{1,0:T(8,128)(2,1)} async-done(((bf16[2048,1024]{1,0:T(8,128)(2,1)}), bf16[512,1024]{1,0:T(8,128)(2,1)}) %reduce-scatter.9.cloned.1.call-update) | async-done | bytes 1048592 | tf_op jit(solution)/shard_map/reduce_scatter | solution.py:256
  529.0 77.0 %reduce-scatter.7.cloned.1.call-done = bf16[512,1024]{1,0:T(8,128)(2,1)} async-done(((bf16[2048,1024]{1,0:T(8,128)(2,1)}), bf16[512,1024]{1,0:T(8,128)(2,1)}) %reduce-scatter.7.cloned.1.call-update) | async-done | bytes 1048592 | tf_op jit(solution)/shard_map/reduce_scatter | solution.py:229
  606.1 4.4 fusion.78
  613.1 11.5 fusion.40
  629.7 5.7 convolution_convert_fusion.5
  635.4 56.5 %all-gather.11.cloned.1.call-done = bf16[2048,1024]{1,0:T(8,128)(2,1)} async-done(((bf16[512,1024]{1,0:T(8,128)(2,1)}), bf16[2048,1024]{1,0:T(8,128)(2,1)}) %all-gather.11.cloned.1.call-update) | async-done | bytes 4194320 | tf_op jit(solution)/shard_map/all_gather | solution.py:267
  691.9 4.4 convolution_convert_fusion.4
  697.4 309.8 %while.45 = (s32[]{:T(128)}, f32[2048,4,64]{0,2,1:T(8,128)}, f32[2048,4,64]{0,2,1:T(8,128)}, f32[4,512,4,64]{1,0,3,2:T(4,128)}, bf16[4,512,4,64]{1,3,2,0:T(8,128...) while((s32[]{:T(128)}, f32[2048,4,64]{0,2,1:T(8,128)}, ...), condition=%wide.region_15.16_spmd.clone, body=%wide.region_13.15_spmd.clone.sunk | while | flops 3303800832 | bytes 259860816 | solution.py:139
  701.4 9.1 fusion.145
  710.5 10.1 fusion.149
  720.6 11.0 fusion.147
  731.6 9.9 multiply_reduce_fusion.3
  741.5 10.7 multiply_convert_fusion.5
  752.2 6.2 fusion.148
  758.4 3.9 fusion.146
  762.9 11.1 dynamic_update_slice.43
  777.8 9.1 fusion.145
  786.9 10.1 fusion.149
  797.0 11.6 fusion.147
  808.5 9.9 multiply_reduce_fusion.3
  818.5 10.7 multiply_convert_fusion.5
  829.2 6.2 fusion.148
  835.4 4.6 fusion.146
  840.5 11.1 dynamic_update_slice.43
  855.5 9.1 fusion.145
  864.5 10.1 fusion.149
  874.7 11.6 fusion.147
  886.2 9.9 multiply_reduce_fusion.3
  896.2 10.7 multiply_convert_fusion.5
  906.8 6.2 fusion.148
  913.0 4.6 fusion.146
  918.2 11.1 dynamic_update_slice.43
  933.2 9.1 fusion.145
  942.2 10.1 fusion.149
  952.3 11.6 fusion.147
  963.9 9.9 multiply_reduce_fusion.3
  973.8 10.7 multiply_convert_fusion.5
  984.5 6.2 fusion.148
  990.7 4.6 fusion.146
  995.9 11.1 dynamic_update_slice.43
  1027.0 6.7 convolution_convert_fusion.2
  1033.7 119.4 %all-reduce.4.cloned.1.call-done = (bf16[1024,256]{1,0:T(8,128)(2,1)}, bf16[1024,256]{1,0:T(8,128)(2,1)}, bf16[1024,256]{1,0:T(8,128)(2,1)}, bf16[256,1024]{1,0:...) async-done(((bf16[1024,256]{1,0:T(8,128)(2,1)}, bf16[1024,256]{1,0:T(8,128)(2,1)}, bf16[1024,256]{1,0:T(8,128)(2,1)}, ...) | async-done | bytes 8388624 | tf_op jit(solution)/shard_map/psum | solution.py:308
  1168.1 64.4 %reduce-scatter.11.cloned.1.call-done = bf16[512,1024]{1,0:T(8,128)(2,1)} async-done(((bf16[2048,1024]{1,0:T(8,128)(2,1)}), bf16[512,1024]{1,0:T(8,128)(2,1)}) %reduce-scatter.11.cloned.1.call-update) | async-done | bytes 1048592 | tf_op jit(solution)/shard_map/reduce_scatter | solution.py:296
  1234.8 41.0 %all-reduce = (f32[1024]{0:T(1024)}, f32[1024]{0:T(1024)}, f32[1024]{0:T(1024)}, f32[1024]{0:T(1024)}) all-reduce(f32[1024]{0:T(1024)S(1)} %get-tuple-element.261, f32[1024]{0:T(1024)S(1)} %get-tuple-element.266, f32[1024]{0:T(1024)S(1)} %copy-done.41, f32[1024]{0:T(1024)S(1)} %copy-done.42), channel_id=1, replica_groups=mesh['dp'=8,'tensor'=4] {'dp','tensor'}, use_global_device_ids=true, to_apply=%region_20.21 | all-reduce | flops 4096 | bytes 32768 | tf_op jit(solution)/shard_map/psum | solution.py:316
  1275.8 3.9 fusion.55
  (228 shorter events, 112.9 us)
Async XLA Ops:
  7.2 414.7 %copy-start = (bf16[1024,1024]{1,0:T(8,128)(2,1)S(1)}, bf16[1024,1024]{1,0:T(8,128)(2,1)}, u32[]{:S(2)}) copy-start(bf16[1024,1024]{1,0:T(8,128)(2,1)} %param.30) | copy-start | bytes 6291460
  7.2 6.7 copy-start.33
  7.2 7.5 copy-start.34
  7.2 90.2 %all-gather.5.cloned.1.call-start = ((), (), s32[]{:S(2)}) async-start(), calls=%async_computation.4 | async-start | bytes 5242880 | tf_op jit(solution)/shard_map/all_gather | solution.py:209
  13.8 240.3 %reduce-scatter.5.cloned.1.call-start = ((), (), s32[]{:S(2)}) async-start(), calls=%async_computation.5 | async-start | bytes 5242880 | tf_op jit(solution)/shard_map/reduce_scatter | solution.py:214
  18.5 86.6 %copy-start.15 = (f32[2048,32]{0,1:T(8,128)}, f32[2048,32]{0,1:T(8,128)S(1)}, u32[]{:S(2)}) copy-start(f32[2048,32]{0,1:T(8,128)S(1)} %get-tuple-element.349) | copy-start | bytes 786436
  18.5 86.6 %copy-start.17 = (f32[2048,32]{0,1:T(8,128)}, f32[2048,32]{0,1:T(8,128)S(1)}, u32[]{:S(2)}) copy-start(f32[2048,32]{0,1:T(8,128)S(1)} %get-tuple-element.350) | copy-start | bytes 786436
  105.8 2.0 copy-start.11
  105.8 2.0 copy-start.13
  105.8 2.0 copy-start.14
  115.5 3.8 copy-start.24
  131.6 3.8 copy-start.24
  147.6 3.8 copy-start.24
  163.6 3.8 copy-start.24
  172.9 2.4 copy-start.30
  178.6 75.5 %copy-start.4 = (bf16[512,1024]{1,0:T(8,128)(2,1)S(1)}, bf16[512,1024]{1,0:T(8,128)(2,1)}, u32[]{:S(2)}) copy-start(bf16[512,1024]{1,0:T(8,128)(2,1)} %param.18) | copy-start | bytes 3145732
  178.6 78.9 %copy-start.37 = (f32[1024]{0:T(1024)S(1)}, f32[1024]{0:T(1024)}, u32[]{:S(2)}) copy-start(f32[1024]{0:T(1024)} %param.26) | copy-start | bytes 12292
  178.6 78.9 %copy-start.43 = (f32[1024]{0:T(1024)S(1)}, f32[1024]{0:T(1024)}, u32[]{:S(2)}) copy-start(f32[1024]{0:T(1024)} %param.27) | copy-start | bytes 12292
  178.7 161.8 %all-gather.7.cloned.1.call-start = ((), (), s32[]{:S(2)}) async-start(), calls=%async_computation.6 | async-start | bytes 5242880 | tf_op jit(solution)/shard_map/all_gather | solution.py:226
  254.1 3.4 copy-start.7
  259.1 162.8 %all-gather.9.cloned.1.call-start = ((), (), s32[]{:S(2)}) async-start(), calls=%async_computation.8 | async-start | bytes 5242880 | tf_op jit(solution)/shard_map/all_gather | solution.py:240
  262.3 263.8 %reduce-scatter.9.cloned.1.call-start = ((), (), s32[]{:S(2)}) async-start(), calls=%async_computation.9 | async-start | bytes 5242880 | tf_op jit(solution)/shard_map/reduce_scatter | solution.py:256
  262.3 3.2 copy-start.23
  435.2 2.0 copy-start.49
  435.2 3.3 copy-start.50
  450.6 155.5 %reduce-scatter.7.cloned.1.call-start = ((), (), s32[]{:S(2)}) async-start(), calls=%async_computation.7 | async-start | bytes 5242880 | tf_op jit(solution)/shard_map/reduce_scatter | solution.py:229
  459.4 66.7 %copy-start.8 = (bf16[512,1024]{1,0:T(8,128)(2,1)S(1)}, bf16[512,1024]{1,0:T(8,128)(2,1)}, u32[]{:S(2)}) copy-start(bf16[512,1024]{1,0:T(8,128)(2,1)} %reduce-scatter.5.cloned.1.call-done) | copy-start | bytes 3145732
  459.4 232.5 %all-gather.11.cloned.1.call-start = ((), (), s32[]{:S(2)}) async-start(), calls=%async_computation.10 | async-start | bytes 5242880 | tf_op jit(solution)/shard_map/all_gather | solution.py:267
  529.0 81.5 %copy-start.10 = (bf16[1,2048,4,32]{1,3,2,0:T(8,128)(2,1)S(1)}, bf16[1,2048,4,32]{1,3,2,0:T(8,128)(2,1)}, u32[]{:S(2)}) copy-start(bf16[1,2048,4,32]{1,3,2,0:T(8,128)(2,1)} %copy-done.9) | copy-start | bytes 1572868
  529.0 81.5 %copy-start.12 = (bf16[1,2048,4,32]{1,3,2,0:T(8,128)(2,1)S(1)}, bf16[1,2048,4,32]{1,3,2,0:T(8,128)(2,1)}, u32[]{:S(2)}) copy-start(bf16[1,2048,4,32]{1,3,2,0:T(8,128)(2,1)} %copy-done.11) | copy-start | bytes 1572868
  610.5 542.6 %all-reduce.4.cloned.1.call-start = ((), (), s32[]{:S(2)}) async-start(), calls=%async_computation.12 | async-start | bytes 16777216 | tf_op jit(solution)/shard_map/psum | solution.py:308
  610.5 2.6 copy-start.46
  624.7 3.7 copy-start.47
  624.7 5.0 copy-start.48
  629.7 62.2 %copy-start.31 = (bf16[256,1024]{1,0:T(8,128)(2,1)S(1)}, bf16[256,1024]{1,0:T(8,128)(2,1)}, u32[]{:S(2)}) copy-start(bf16[256,1024]{1,0:T(8,128)(2,1)} %param.25) | copy-start | bytes 1572868
  720.6 11.0 copy-start.2
  752.2 6.2 copy-start.3
  797.0 11.6 copy-start.2
  829.2 6.2 copy-start.3
  874.7 11.6 copy-start.2
  906.8 6.2 copy-start.3
  952.3 11.6 copy-start.2
  984.5 6.2 copy-start.3
  1007.2 3.5 copy-start.22
  1010.6 4.8 copy-start.6
  1010.6 4.8 copy-start.16
  1010.6 4.8 copy-start.18
  1015.5 2.5 copy-start.25
  1015.5 3.1 copy-start.44
  1018.0 4.2 copy-start.27
  1018.6 4.7 copy-start.29
  1018.6 4.7 copy-start.45
  1025.4 207.1 %reduce-scatter.11.cloned.1.call-start = ((), (), s32[]{:S(2)}) async-start(), calls=%async_computation.11 | async-start | bytes 5242880 | tf_op jit(solution)/shard_map/reduce_scatter | solution.py:296
  1153.1 6.4 copy-start.32
  1153.1 7.5 copy-start.21
  1159.5 3.6 copy-start.20
  1163.1 2.5 copy-start.19
  1165.5 67.0 %copy-start.5 = (bf16[512,1024]{1,0:T(8,128)(2,1)S(1)}, bf16[512,1024]{1,0:T(8,128)(2,1)}, u32[]{:S(2)}) copy-start(bf16[512,1024]{1,0:T(8,128)(2,1)} %param.18) | copy-start | bytes 3145732
  1165.5 67.0 %copy-start.36 = (f32[512]{0:T(512)S(1)}, f32[512]{0:T(512)}, u32[]{:S(2)}) copy-start(f32[512]{0:T(512)} %copy-done.35) | copy-start | bytes 6148
  1165.5 67.0 %copy-start.38 = (f32[1024]{0:T(1024)S(1)}, f32[1024]{0:T(1024)}, u32[]{:S(2)}) copy-start(f32[1024]{0:T(1024)} %param.20) | copy-start | bytes 12292
  1165.5 67.0 %copy-start.40 = (f32[512]{0:T(512)S(1)}, f32[512]{0:T(512)}, u32[]{:S(2)}) copy-start(f32[512]{0:T(512)} %copy-done.39) | copy-start | bytes 6148
  1165.6 69.2 %copy-start.41 = (f32[1024]{0:T(1024)S(1)}, f32[1024]{0:T(1024)}, u32[]{:S(2)}) copy-start(f32[1024]{0:T(1024)} %get-tuple-element.259) | copy-start | bytes 12292
  1165.6 69.2 %copy-start.42 = (f32[1024]{0:T(1024)S(1)}, f32[1024]{0:T(1024)}, u32[]{:S(2)}) copy-start(f32[1024]{0:T(1024)} %get-tuple-element.265) | copy-start | bytes 12292
  1165.6 114.2 %copy-start.1 = (bf16[1024,1024]{1,0:T(8,128)(2,1)S(1)}, bf16[1024,1024]{1,0:T(8,128)(2,1)}, u32[]{:S(2)}) copy-start(bf16[1024,1024]{1,0:T(8,128)(2,1)} %param.30) | copy-start | bytes 6291460
  (5 other events, 5.8 us)
Sparse Core Ops, SparseCore 0:
  13.9 83.4 all-gather.4
  178.8 75.2 reduce-scatter.4
  259.2 81.2 all-gather.6
  342.6 79.2 all-gather.8
  450.7 75.2 reduce-scatter.8
  528.8 77.2 reduce-scatter.6
  610.6 81.2 all-gather.10
  1025.6 127.4 all-reduce.3
  1155.4 77.0 reduce-scatter.10
where the time goes:
time: 1300 us; the launch traced here: 1290 us
  waiting for transfers between devices  668 us (51%)
  matrix products  333 us (26%)
  other arithmetic  114 us (9%)
  local copies, waits for them, and re-layouts  86.1 us (7%)
  blocking collectives  41 us (3%)
  loops' own time  18.8 us (1%)
  between operations  15.5 us (1%)
    psum x1, waiting for transfers between devices, on_device(): lax.psum(query_grad.astype(jnp.bfloat16), 'dp').astype(jnp.float32)  119 us
    all_gather x1, waiting for transfers between devices, on_device(): attn_rows = lax.all_gather(attn_in, 'tensor', axis=0, tiled=True)  78.9 us
    reduce_scatter x1, waiting for transfers between devices, on_device(): lax.psum_scatter(jnp.dot(picked, down_weight, preferred_element_type=jnp....  77 us
    all_gather x1, waiting for transfers between devices, on_device(): ffn_rows = lax.all_gather(ffn_in, 'tensor', axis=0, tiled=True)  73.5 us
    reduce_scatter x1, waiting for transfers between devices, on_device(): lax.psum_scatter(jnp.einsum('rf,df->rd', picked, w_pair, preferred_elemen...  66.6 us
    all_gather x1, waiting for transfers between devices, on_device(): lax.all_gather(grad_out.astype(jnp.bfloat16), 'tensor', axis=0, tiled=True)  66.2 us
    reduce_scatter x1, waiting for transfers between devices, on_device(): lax.psum_scatter(jnp.dot(picked, w_out, preferred_element_type=jnp.float3...  65.3 us
    reduce_scatter x1, waiting for transfers between devices, on_device(): lax.psum_scatter(jnp.einsum('rc,dc->rd', picked, w_qkv, preferred_element...  64.4 us
  transfers between devices with their start and end apart: 9, of which 9 were waited for; matrix products, arithmetic and copies ran while one was open for 6% of the time, Pallas kernels for 0%

commit v1 on v0

--- a/solution.py
+++ b/solution.py
@@ -314,7 +314,7 @@
         lax.psum(down_grad.astype(jnp.bfloat16), "dp").astype(jnp.float32),
     )
     gain1_grad, shift1_grad, gain2_grad, shift2_grad = lax.psum(
-        (gain1_grad, shift1_grad, gain2_grad, shift2_grad), ("dp", "tensor")
+        lax.psum((gain1_grad, shift1_grad, gain2_grad, shift2_grad), "tensor"), "dp"
     )
     return (
         output,

time: 1300 us -> 1300 us (level)
    psum x1 -> x2, blocking collectives: 41 us -> 40.8 us  [the longest x1 22.9 us: on_device(): lax.psum(lax.psum((gain1_grad, shift1_grad, gain2_grad, shift2_grad), 'te...]
where the time goes in v1:
time: 1300 us; the launch traced here: 1290 us
  waiting for transfers between devices  668 us (51%)
  matrix products  333 us (26%)
  other arithmetic  114 us (9%)
  local copies, waits for them, and re-layouts  86.2 us (7%)
  blocking collectives  40.8 us (3%)
  loops' own time  18.8 us (1%)
  between operations  15.5 us (1%)
    psum x1, waiting for transfers between devices, on_device(): lax.psum(query_grad.astype(jnp.bfloat16), 'dp').astype(jnp.float32)  119 us
    all_gather x1, waiting for transfers between devices, on_device(): attn_rows = lax.all_gather(attn_in, 'tensor', axis=0, tiled=True)  78.9 us
    reduce_scatter x1, waiting for transfers between devices, on_device(): lax.psum_scatter(jnp.dot(picked, down_weight, preferred_element_type=jnp....  77 us
    all_gather x1, waiting for transfers between devices, on_device(): ffn_rows = lax.all_gather(ffn_in, 'tensor', axis=0, tiled=True)  73.5 us
    reduce_scatter x1, waiting for transfers between devices, on_device(): lax.psum_scatter(jnp.einsum('rf,df->rd', picked, w_pair, preferred_elemen...  66.6 us
    all_gather x1, waiting for transfers between devices, on_device(): lax.all_gather(grad_out.astype(jnp.bfloat16), 'tensor', axis=0, tiled=True)  66.2 us
    reduce_scatter x1, waiting for transfers between devices, on_device(): lax.psum_scatter(jnp.dot(picked, w_out, preferred_element_type=jnp.float3...  65.3 us
    reduce_scatter x1, waiting for transfers between devices, on_device(): lax.psum_scatter(jnp.einsum('rc,dc->rd', picked, w_qkv, preferred_element...  64.4 us
  transfers between devices with their start and end apart: 9, of which 9 were waited for; matrix products, arithmetic and copies ran while one was open for 6% of the time, Pallas kernels for 0%

profile of v1, /device:TPU:0, one launch (start us, length us, event | category | flops | bytes accessed | tf_op | source)
XLA Modules:
  0.0 1286.5 jit_solution(6158226885694271942)
XLA Ops:
  18.5 78.9 %all-gather.5.cloned.1.call-done = bf16[2048,1024]{1,0:T(8,128)(2,1)} async-done(((bf16[512,1024]{1,0:T(8,128)(2,1)}), bf16[2048,1024]{1,0:T(8,128)(2,1)}) %all-gather.5.cloned.1.call-update) | async-done | bytes 4194320 | tf_op jit(solution)/shard_map/all_gather | solution.py:209
  97.4 5.8 fusion.82
  108.9 64.1 %while.44 = (s32[]{:T(128)}, bf16[4,512,4,64]{1,3,2,0:T(8,128)(2,1)}, f32[4,4,512]{2,1,0:T(4,128)S(1)}, s32[1]{0:T(128)}, s32[4]{0:T(128)S(1)}, /*index=5*/bf16[...) while((s32[]{:T(128)}, ...), condition=%wide.region_5.6_spmd, body=%wide.region_2.5_spmd.sunk | while | flops 1124204544 | bytes 57221472 | solution.py:86
  115.6 3.7 fusion.132
  119.3 5.5 fusion.133
  131.6 3.7 fusion.132
  135.3 5.5 fusion.133
  151.4 5.5 fusion.133
  163.6 3.7 fusion.132
  167.4 5.5 fusion.133
  178.7 10.1 all-gather.7.cloned.1.call-start
  188.8 65.3 %reduce-scatter.5.cloned.1.call-done = bf16[512,1024]{1,0:T(8,128)(2,1)} async-done(((bf16[2048,1024]{1,0:T(8,128)(2,1)}), bf16[512,1024]{1,0:T(8,128)(2,1)}) %reduce-scatter.5.cloned.1.call-update) | async-done | bytes 1048592 | tf_op jit(solution)/shard_map/reduce_scatter | solution.py:214
  267.0 73.5 %all-gather.7.cloned.1.call-done = bf16[2048,1024]{1,0:T(8,128)(2,1)} async-done(((bf16[512,1024]{1,0:T(8,128)(2,1)}), bf16[2048,1024]{1,0:T(8,128)(2,1)}) %all-gather.7.cloned.1.call-update) | async-done | bytes 4194320 | tf_op jit(solution)/shard_map/all_gather | solution.py:226
  340.5 15.2 %fusion.83 = f32[2048,2048]{0,1:T(8,128)} fusion(bf16[2048,1024]{1,0:T(8,128)(2,1)} %all-gather.7.cloned.1.call-done, bf16[1024,2048]{1,0:T(8,128)(2,1)} %constant_dynamic-update-slice_fusion.3), kind=kOutput, calls=%fused_computation.160 | convolution fusion | flops 8589934592 | bytes 25165824 | tf_op jit(solution)/shard_map/dot_general | solution.py:200
  355.7 66.2 %all-gather.9.cloned.1.call-done = bf16[2048,1024]{1,0:T(8,128)(2,1)} async-done(((bf16[512,1024]{1,0:T(8,128)(2,1)}), bf16[2048,1024]{1,0:T(8,128)(2,1)}) %all-gather.9.cloned.1.call-update) | async-done | bytes 4194320 | tf_op jit(solution)/shard_map/all_gather | solution.py:240
  421.9 13.3 %multiply_convert_fusion.2 = (bf16[2048,1024]{0,1:T(8,128)(2,1)S(1)}, bf16[2048,1024]{0,1:T(8,128)(2,1)S(1)}, bf16[2048,1024]{0,1:T(8,128)(2,1)}) fusion(f32[2048,2048]{0,1:T(8,128)} %fusion.83, bf16[2048,1024]{1,0:T(8,128)(2,1)} %all-gather.9.cloned.1.call-done, bf16[1024,1024]{1,0:T(8,128)(2,1)S(1)} %copy-done), kind=kOutput, calls=%fused_computation.51 | convolution fusion | flops 4328521728 | bytes 35651584 | tf_op jit(solution)/shard_map/rd,fd->rf/dot_general | solution.py:246
  438.5 12.1 fusion.39
  450.6 8.7 convolution_convert_fusion.3
  459.4 66.6 %reduce-scatter.9.cloned.1.call-done = bf16[512,1024]{1,0:T(8,128)(2,1)} async-done(((bf16[2048,1024]{1,0:T(8,128)(2,1)}), bf16[512,1024]{1,0:T(8,128)(2,1)}) %reduce-scatter.9.cloned.1.call-update) | async-done | bytes 1048592 | tf_op jit(solution)/shard_map/reduce_scatter | solution.py:256
  529.0 77.0 %reduce-scatter.7.cloned.1.call-done = bf16[512,1024]{1,0:T(8,128)(2,1)} async-done(((bf16[2048,1024]{1,0:T(8,128)(2,1)}), bf16[512,1024]{1,0:T(8,128)(2,1)}) %reduce-scatter.7.cloned.1.call-update) | async-done | bytes 1048592 | tf_op jit(solution)/shard_map/reduce_scatter | solution.py:229
  606.1 4.4 fusion.78
  613.1 11.5 fusion.40
  629.7 5.7 convolution_convert_fusion.5
  635.4 56.5 %all-gather.11.cloned.1.call-done = bf16[2048,1024]{1,0:T(8,128)(2,1)} async-done(((bf16[512,1024]{1,0:T(8,128)(2,1)}), bf16[2048,1024]{1,0:T(8,128)(2,1)}) %all-gather.11.cloned.1.call-update) | async-done | bytes 4194320 | tf_op jit(solution)/shard_map/all_gather | solution.py:267
  691.9 4.4 convolution_convert_fusion.4
  697.4 309.8 %while.45 = (s32[]{:T(128)}, f32[2048,4,64]{0,2,1:T(8,128)}, f32[2048,4,64]{0,2,1:T(8,128)}, f32[4,512,4,64]{1,0,3,2:T(4,128)}, bf16[4,512,4,64]{1,3,2,0:T(8,128...) while((s32[]{:T(128)}, f32[2048,4,64]{0,2,1:T(8,128)}, ...), condition=%wide.region_15.16_spmd.clone, body=%wide.region_13.15_spmd.clone.sunk | while | flops 3303800832 | bytes 259860816 | solution.py:139
  701.4 9.1 fusion.145
  710.5 10.1 fusion.149
  720.6 11.0 fusion.147
  731.6 9.9 multiply_reduce_fusion.3
  741.5 10.7 multiply_convert_fusion.5
  752.2 6.2 fusion.148
  758.4 3.9 fusion.146
  762.8 11.1 dynamic_update_slice.43
  777.8 9.1 fusion.145
  786.9 10.1 fusion.149
  797.0 11.6 fusion.147
  808.5 9.9 multiply_reduce_fusion.3
  818.4 10.7 multiply_convert_fusion.5
  829.2 6.2 fusion.148
  835.4 4.6 fusion.146
  840.5 11.1 dynamic_update_slice.43
  855.5 9.1 fusion.145
  864.5 10.1 fusion.149
  874.7 11.6 fusion.147
  886.2 9.9 multiply_reduce_fusion.3
  896.1 10.7 multiply_convert_fusion.5
  906.8 6.2 fusion.148
  913.0 4.6 fusion.146
  918.2 11.1 dynamic_update_slice.43
  933.2 9.1 fusion.145
  942.2 10.1 fusion.149
  952.3 11.6 fusion.147
  963.9 9.9 multiply_reduce_fusion.3
  973.8 10.7 multiply_convert_fusion.5
  984.5 6.2 fusion.148
  990.7 4.6 fusion.146
  995.9 11.1 dynamic_update_slice.43
  1027.0 6.7 convolution_convert_fusion.2
  1033.7 119.4 %all-reduce.5.cloned.1.call-done = (bf16[1024,256]{1,0:T(8,128)(2,1)}, bf16[1024,256]{1,0:T(8,128)(2,1)}, bf16[1024,256]{1,0:T(8,128)(2,1)}, bf16[256,1024]{1,0:...) async-done(((bf16[1024,256]{1,0:T(8,128)(2,1)}, bf16[1024,256]{1,0:T(8,128)(2,1)}, bf16[1024,256]{1,0:T(8,128)(2,1)}, ...) | async-done | bytes 8388624 | tf_op jit(solution)/shard_map/psum | solution.py:308
  1168.1 64.4 %reduce-scatter.11.cloned.1.call-done = bf16[512,1024]{1,0:T(8,128)(2,1)} async-done(((bf16[2048,1024]{1,0:T(8,128)(2,1)}), bf16[512,1024]{1,0:T(8,128)(2,1)}) %reduce-scatter.11.cloned.1.call-update) | async-done | bytes 1048592 | tf_op jit(solution)/shard_map/reduce_scatter | solution.py:296
  1234.8 17.9 %all-reduce.1 = (f32[1024]{0:T(1024)S(1)}, f32[1024]{0:T(1024)S(1)}, f32[1024]{0:T(1024)S(1)}, f32[1024]{0:T(1024)S(1)}) all-reduce(f32[1024]{0:T(1024)S(1)} %get-tuple-element.261, f32[1024]{0:T(1024)S(1)} %get-tuple-element.266, f32[1024]{0:T(1024)S(1)} %copy-done.41, ...), channel_id=1, replica_groups=mesh['dp'=8,'tensor'=4] {'tensor'}, use_global_device_ids=true, to_apply=%region_20.21 | all-reduce | flops 4096 | bytes 32768 | tf_op jit(solution)/shard_map/psum | solution.py:317
  1252.7 22.9 %all-reduce = (f32[1024]{0:T(1024)}, f32[1024]{0:T(1024)}, f32[1024]{0:T(1024)}, f32[1024]{0:T(1024)}) all-reduce(f32[1024]{0:T(1024)S(1)} %get-tuple-element.311, f32[1024]{0:T(1024)S(1)} %get-tuple-element.312, f32[1024]{0:T(1024)S(1)} %get-tuple-element.313, ...), channel_id=1, replica_groups=mesh['dp'=8,'tensor'=4] {'dp'}, use_global_device_ids=true, to_apply=%region_21.22 | all-reduce | flops 4096 | bytes 32768 | tf_op jit(solution)/shard_map/psum | solution.py:316
  1275.6 3.9 fusion.55
  (229 shorter events, 116.6 us)
Async XLA Ops:
  7.2 414.7 %copy-start = (bf16[1024,1024]{1,0:T(8,128)(2,1)S(1)}, bf16[1024,1024]{1,0:T(8,128)(2,1)}, u32[]{:S(2)}) copy-start(bf16[1024,1024]{1,0:T(8,128)(2,1)} %param.30) | copy-start | bytes 6291460
  7.2 6.7 copy-start.33
  7.2 7.5 copy-start.34
  7.2 90.2 %all-gather.5.cloned.1.call-start = ((), (), s32[]{:S(2)}) async-start(), calls=%async_computation.4 | async-start | bytes 5242880 | tf_op jit(solution)/shard_map/all_gather | solution.py:209
  13.8 240.3 %reduce-scatter.5.cloned.1.call-start = ((), (), s32[]{:S(2)}) async-start(), calls=%async_computation.5 | async-start | bytes 5242880 | tf_op jit(solution)/shard_map/reduce_scatter | solution.py:214
  18.5 86.6 %copy-start.15 = (f32[2048,32]{0,1:T(8,128)}, f32[2048,32]{0,1:T(8,128)S(1)}, u32[]{:S(2)}) copy-start(f32[2048,32]{0,1:T(8,128)S(1)} %get-tuple-element.353) | copy-start | bytes 786436
  18.5 86.6 %copy-start.17 = (f32[2048,32]{0,1:T(8,128)}, f32[2048,32]{0,1:T(8,128)S(1)}, u32[]{:S(2)}) copy-start(f32[2048,32]{0,1:T(8,128)S(1)} %get-tuple-element.354) | copy-start | bytes 786436
  105.8 2.0 copy-start.11
  105.8 2.0 copy-start.13
  105.8 2.0 copy-start.14
  115.5 3.8 copy-start.24
  131.6 3.8 copy-start.24
  147.6 3.8 copy-start.24
  163.6 3.8 copy-start.24
  172.9 2.4 copy-start.30
  178.6 75.5 %copy-start.4 = (bf16[512,1024]{1,0:T(8,128)(2,1)S(1)}, bf16[512,1024]{1,0:T(8,128)(2,1)}, u32[]{:S(2)}) copy-start(bf16[512,1024]{1,0:T(8,128)(2,1)} %param.18) | copy-start | bytes 3145732
  178.6 78.9 %copy-start.37 = (f32[1024]{0:T(1024)S(1)}, f32[1024]{0:T(1024)}, u32[]{:S(2)}) copy-start(f32[1024]{0:T(1024)} %param.26) | copy-start | bytes 12292
  178.6 78.9 %copy-start.43 = (f32[1024]{0:T(1024)S(1)}, f32[1024]{0:T(1024)}, u32[]{:S(2)}) copy-start(f32[1024]{0:T(1024)} %param.27) | copy-start | bytes 12292
  178.7 161.8 %all-gather.7.cloned.1.call-start = ((), (), s32[]{:S(2)}) async-start(), calls=%async_computation.6 | async-start | bytes 5242880 | tf_op jit(solution)/shard_map/all_gather | solution.py:226
  254.1 3.4 copy-start.7
  259.1 162.8 %all-gather.9.cloned.1.call-start = ((), (), s32[]{:S(2)}) async-start(), calls=%async_computation.8 | async-start | bytes 5242880 | tf_op jit(solution)/shard_map/all_gather | solution.py:240
  262.3 263.8 %reduce-scatter.9.cloned.1.call-start = ((), (), s32[]{:S(2)}) async-start(), calls=%async_computation.9 | async-start | bytes 5242880 | tf_op jit(solution)/shard_map/reduce_scatter | solution.py:256
  262.3 3.2 copy-start.23
  435.2 2.0 copy-start.49
  435.2 3.3 copy-start.50
  450.6 155.5 %reduce-scatter.7.cloned.1.call-start = ((), (), s32[]{:S(2)}) async-start(), calls=%async_computation.7 | async-start | bytes 5242880 | tf_op jit(solution)/shard_map/reduce_scatter | solution.py:229
  459.4 66.7 %copy-start.8 = (bf16[512,1024]{1,0:T(8,128)(2,1)S(1)}, bf16[512,1024]{1,0:T(8,128)(2,1)}, u32[]{:S(2)}) copy-start(bf16[512,1024]{1,0:T(8,128)(2,1)} %reduce-scatter.5.cloned.1.call-done) | copy-start | bytes 3145732
  459.4 232.5 %all-gather.11.cloned.1.call-start = ((), (), s32[]{:S(2)}) async-start(), calls=%async_computation.10 | async-start | bytes 5242880 | tf_op jit(solution)/shard_map/all_gather | solution.py:267
  529.0 81.5 %copy-start.10 = (bf16[1,2048,4,32]{1,3,2,0:T(8,128)(2,1)S(1)}, bf16[1,2048,4,32]{1,3,2,0:T(8,128)(2,1)}, u32[]{:S(2)}) copy-start(bf16[1,2048,4,32]{1,3,2,0:T(8,128)(2,1)} %copy-done.9) | copy-start | bytes 1572868
  529.0 81.5 %copy-start.12 = (bf16[1,2048,4,32]{1,3,2,0:T(8,128)(2,1)S(1)}, bf16[1,2048,4,32]{1,3,2,0:T(8,128)(2,1)}, u32[]{:S(2)}) copy-start(bf16[1,2048,4,32]{1,3,2,0:T(8,128)(2,1)} %copy-done.11) | copy-start | bytes 1572868
  610.4 542.6 %all-reduce.5.cloned.1.call-start = ((), (), s32[]{:S(2)}) async-start(), calls=%async_computation.12 | async-start | bytes 16777216 | tf_op jit(solution)/shard_map/psum | solution.py:308
  610.5 2.6 copy-start.46
  624.7 3.7 copy-start.47
  624.7 5.0 copy-start.48
  629.7 62.2 %copy-start.31 = (bf16[256,1024]{1,0:T(8,128)(2,1)S(1)}, bf16[256,1024]{1,0:T(8,128)(2,1)}, u32[]{:S(2)}) copy-start(bf16[256,1024]{1,0:T(8,128)(2,1)} %param.25) | copy-start | bytes 1572868
  720.6 11.0 copy-start.2
  752.2 6.2 copy-start.3
  797.0 11.6 copy-start.2
  829.2 6.2 copy-start.3
  874.7 11.6 copy-start.2
  906.8 6.2 copy-start.3
  952.3 11.6 copy-start.2
  984.5 6.2 copy-start.3
  1007.2 3.5 copy-start.22
  1010.6 4.8 copy-start.6
  1010.6 4.8 copy-start.16
  1010.6 4.8 copy-start.18
  1015.5 2.5 copy-start.25
  1015.5 3.1 copy-start.44
  1018.0 4.2 copy-start.27
  1018.6 4.7 copy-start.29
  1018.6 4.7 copy-start.45
  1025.4 207.1 %reduce-scatter.11.cloned.1.call-start = ((), (), s32[]{:S(2)}) async-start(), calls=%async_computation.11 | async-start | bytes 5242880 | tf_op jit(solution)/shard_map/reduce_scatter | solution.py:296
  1153.1 6.4 copy-start.32
  1153.1 7.5 copy-start.21
  1159.5 3.6 copy-start.20
  1163.1 2.5 copy-start.19
  1165.5 67.0 %copy-start.5 = (bf16[512,1024]{1,0:T(8,128)(2,1)S(1)}, bf16[512,1024]{1,0:T(8,128)(2,1)}, u32[]{:S(2)}) copy-start(bf16[512,1024]{1,0:T(8,128)(2,1)} %param.18) | copy-start | bytes 3145732
  1165.5 67.0 %copy-start.36 = (f32[512]{0:T(512)S(1)}, f32[512]{0:T(512)}, u32[]{:S(2)}) copy-start(f32[512]{0:T(512)} %copy-done.35) | copy-start | bytes 6148
  1165.5 67.0 %copy-start.38 = (f32[1024]{0:T(1024)S(1)}, f32[1024]{0:T(1024)}, u32[]{:S(2)}) copy-start(f32[1024]{0:T(1024)} %param.20) | copy-start | bytes 12292
  1165.5 67.0 %copy-start.40 = (f32[512]{0:T(512)S(1)}, f32[512]{0:T(512)}, u32[]{:S(2)}) copy-start(f32[512]{0:T(512)} %copy-done.39) | copy-start | bytes 6148
  1165.6 69.2 %copy-start.41 = (f32[1024]{0:T(1024)S(1)}, f32[1024]{0:T(1024)}, u32[]{:S(2)}) copy-start(f32[1024]{0:T(1024)} %get-tuple-element.259) | copy-start | bytes 12292
  1165.6 69.2 %copy-start.42 = (f32[1024]{0:T(1024)S(1)}, f32[1024]{0:T(1024)}, u32[]{:S(2)}) copy-start(f32[1024]{0:T(1024)} %get-tuple-element.265) | copy-start | bytes 12292
  1165.6 114.0 %copy-start.1 = (bf16[1024,1024]{1,0:T(8,128)(2,1)S(1)}, bf16[1024,1024]{1,0:T(8,128)(2,1)}, u32[]{:S(2)}) copy-start(bf16[1024,1024]{1,0:T(8,128)(2,1)} %param.30) | copy-start | bytes 6291460
  (5 other events, 5.8 us)
Sparse Core Ops, SparseCore 0:
  13.9 83.4 all-gather.4
  178.8 75.2 reduce-scatter.4
  259.2 81.2 all-gather.6
  342.6 79.2 all-gather.8
  450.7 75.2 reduce-scatter.8
  528.8 77.2 reduce-scatter.6
  610.6 81.2 all-gather.10
  1025.6 127.4 all-reduce.4
  1155.4 77.0 reduce-scatter.10
